TPU v7x, 32 devices: a whole 2x2x4 slice. The times are simulated.
32 devices in a mesh: batch: 4 (over z), seq: 4 (over y, core), head: 2 (over x).
Axes of the slice: x: 2, y: 2, z: 4, core: 2. Of those that a mesh axis runs over, the one named last changes fastest.
Arguments:
- image_hidden: bfloat16 [8, 1024, 3072], P('batch', 'seq', 'head'), parts along dimension 0, may hold values from -6 to 6
- modulation: float32 [8, 3, 3072], P('batch'), parts along dimension 0, may hold values from -4 to 4
- qkv_weight: bfloat16 [3072, 3, 1536], P(None, None, 'head'), may hold values from -0.109375 to 0.109375
- out_weight: bfloat16 [1536, 3072], P('head'), may hold values from -0.15625 to 0.15625
- q_gain: float32 [128], replicated, may hold values from 1.2 to 2.5
- k_gain: float32 [128], replicated, may hold values from 1.2 to 2.5
- text_keys: bfloat16 [8, 128, 1536], P('batch', 'seq', 'head'), parts along dimension 0, may hold values from -10 to 10
- text_values: bfloat16 [8, 128, 1536], P('batch', 'seq', 'head'), parts along dimension 0, may hold values from -6 to 6
- stale_keys: bfloat16 [8, 1024, 1536], P('batch', 'seq', 'head'), parts along dimension 0, may hold values from -64 to 64
- stale_values: bfloat16 [8, 1024, 1536], P('batch', 'seq', 'head'), parts along dimension 0, may hold values from -6 to 6
- cached_residual: bfloat16 [8, 1024, 3072], P('batch', 'seq', 'head'), parts along dimension 0, may hold values from -6 to 6
- patch_of: int32 [16], P('batch'), parts along dimension 0, may hold values from 0 to 3, each once
- refresh: int32 [16], P('batch'), parts along dimension 0, may hold values from 0 to 1, as said below
- text_len: int32 [8], P('batch'), parts along dimension 0, may hold values from 16 to 128
Outputs:
- image_out: bfloat16 [8, 1024, 3072], P('batch', 'seq', 'head'), parts along dimension 0
There are 4 independent parts, one for each index of `batch`. A program takes and returns all parts, laid end to end along the dimension named above; an argument that names none is the same for every part. Nothing has to cross between parts.
Inputs may be any that keep to these rules, and one draw needn't show every extreme that they name: `patch_of`: A permutation: every image band sits on exactly one index of seq. `refresh`: exactly 1 entries are 1, the rest 0.
All inputs are finite; a program needn't handle non-finite values.
Results may differ from a plain program's by a relative error of at most 0.012.
The roundings to bfloat16 on the way count: a program that leaves them out, or rounds other values in their place, can miss the bound.
Values may be sent and summed in bfloat16 or wider, within the bound.
A program may use at most 192 MiB of HBM per device.

v0:
```python
import jax
import jax.numpy as jnp
from jax import lax
from jax.sharding import PartitionSpec as P

GRID_W = 64
epsilon = 1e-06


def rotary_tables(raster, head_dim, grid_width):
    half_dim = head_dim // 2
    first_pairs = head_dim // 16
    axis_pairs = (half_dim - first_pairs) // 2
    pair_index = jnp.arange(half_dim, dtype=jnp.int32)
    pair_local = jnp.where(
        pair_index < first_pairs + axis_pairs,
        pair_index - first_pairs,
        pair_index - first_pairs - axis_pairs,
    )
    exponent = -pair_local.astype(jnp.float32) / float(axis_pairs)
    frequency = jnp.where(
        pair_index < first_pairs, jnp.float32(0.0), jnp.power(jnp.float32(10000.0), exponent)
    )
    row_pos = (raster // grid_width).astype(jnp.float32)
    col_pos = (raster % grid_width).astype(jnp.float32)
    position = jnp.where(
        pair_index[None, :] < first_pairs + axis_pairs, row_pos[:, None], col_pos[:, None]
    )
    angles = position * frequency[None, :]
    cosine = jnp.cos(angles)
    sine = jnp.sin(angles)
    return (jnp.concatenate([cosine, cosine], axis=-1), jnp.concatenate([-sine, sine], axis=-1))


def rms_rotate(vectors, gain_vec, cos_full, sin_full):
    scaled = (
        vectors
        * lax.rsqrt(jnp.mean(vectors * vectors, axis=-1, keepdims=True) + epsilon)
        * gain_vec
    )
    half_dim = vectors.shape[-1] // 2
    return (
        scaled * cos_full[None, :, None, :]
        + jnp.roll(scaled, half_dim, axis=-1) * sin_full[None, :, None, :]
    )


def per_device(
    image_hidden,
    modulation,
    qkv_weight,
    out_weight,
    q_gain,
    k_gain,
    text_keys,
    text_values,
    stale_keys,
    stale_values,
    cached_residual,
    patch_of,
    refresh,
    text_len,
):
    prompts, tok_rows, width_part = image_hidden.shape
    head_dim = q_gain.shape[0]
    channels = out_weight.shape[0]
    local_heads = channels // head_dim
    seq_seat = lax.axis_index("seq")
    head_seat = lax.axis_index("head")
    gathered = lax.all_gather(image_hidden, "head", axis=2, tiled=True)
    model_width = gathered.shape[2]
    hidden_f32 = gathered.astype(jnp.float32)
    row_mean = jnp.mean(hidden_f32, axis=-1, keepdims=True)
    centered = hidden_f32 - row_mean
    variance = jnp.mean(centered * centered, axis=-1, keepdims=True)
    normed = centered * lax.rsqrt(variance + epsilon)
    modulated = (
        normed * (1.0 + modulation[:, 1][:, None, :]) + modulation[:, 0][:, None, :]
    ).astype(jnp.bfloat16)
    projected = jnp.dot(
        modulated.reshape(prompts * tok_rows, model_width),
        qkv_weight.reshape(model_width, 3 * channels),
        preferred_element_type=jnp.float32,
    )
    projected = projected.reshape(prompts, tok_rows, 3, local_heads, head_dim)
    seat_ids = jnp.arange(patch_of.shape[0], dtype=jnp.int32)
    own_band = jnp.sum(jnp.where(seat_ids == seq_seat, patch_of, 0))
    own_flag = jnp.sum(jnp.where(seat_ids == seq_seat, refresh, 0))
    raster = own_band * tok_rows + jnp.arange(tok_rows, dtype=jnp.int32)
    cos_full, sin_full = rotary_tables(raster, head_dim, GRID_W)
    fresh_q = rms_rotate(projected[:, :, 0], q_gain, cos_full, sin_full).astype(jnp.bfloat16)
    fresh_k = rms_rotate(projected[:, :, 1], k_gain, cos_full, sin_full).astype(jnp.bfloat16)
    fresh_v = projected[:, :, 2].astype(jnp.bfloat16)
    fresh_k_flat = fresh_k.reshape(prompts, tok_rows, channels)
    fresh_v_flat = fresh_v.reshape(prompts, tok_rows, channels)
    score_scale = head_dim ** (-0.5)
    text_k, text_v = (
        lax.all_gather(text_keys, "seq", axis=1, tiled=True),
        lax.all_gather(text_values, "seq", axis=1, tiled=True),
    )
    total_text = text_k.shape[1]
    text_key_rows = text_k.reshape(prompts, total_text, local_heads, head_dim)
    text_value_rows = text_v.reshape(prompts, total_text, local_heads, head_dim)
    text_scores = (
        jnp.einsum("pqhd,pkhd->phqk", fresh_q, text_key_rows, preferred_element_type=jnp.float32)
        * score_scale
    )
    text_valid = jnp.arange(total_text, dtype=jnp.int32)[None, :] < text_len[:, None]
    text_scores = jnp.where(text_valid[:, None, None, :], text_scores, -1e30)
    row_top = jnp.max(text_scores, axis=-1)
    text_weights = jnp.exp(text_scores - row_top[..., None])
    row_total = jnp.sum(text_weights, axis=-1)
    weighted = jnp.einsum(
        "phqk,pkhd->phqd",
        text_weights.astype(jnp.bfloat16),
        text_value_rows,
        preferred_element_type=jnp.float32,
    )
    running = (row_top, row_total, weighted)
    chosen_k = jnp.where(own_flag == 1, fresh_k_flat, stale_keys)
    chosen_v = jnp.where(own_flag == 1, fresh_v_flat, stale_values)
    key_rows = lax.all_gather(chosen_k[None], "seq", axis=0, tiled=True)
    value_rows = lax.all_gather(chosen_v[None], "seq", axis=0, tiled=True)
    piece_count = key_rows.shape[0]
    is_mine = jnp.arange(piece_count, dtype=jnp.int32) == seq_seat
    key_rows = jnp.where(is_mine[:, None, None, None], fresh_k_flat[None], key_rows)
    value_rows = jnp.where(is_mine[:, None, None, None], fresh_v_flat[None], value_rows)
    key_rows = key_rows.reshape(piece_count, prompts, tok_rows, local_heads, head_dim)
    value_rows = value_rows.reshape(piece_count, prompts, tok_rows, local_heads, head_dim)
    old_top, old_total, old_weighted = running
    scores = (
        jnp.einsum("pqhd,npkhd->phqnk", fresh_q, key_rows, preferred_element_type=jnp.float32)
        * score_scale
    )
    new_top = jnp.maximum(old_top, jnp.max(scores, axis=(3, 4)))
    shrink = jnp.exp(old_top - new_top)
    weights = jnp.exp(scores - new_top[..., None, None])
    new_total = old_total * shrink + jnp.sum(weights, axis=(3, 4))
    added = jnp.einsum(
        "phqnk,npkhd->phqd",
        weights.astype(jnp.bfloat16),
        value_rows,
        preferred_element_type=jnp.float32,
    )
    running = (new_top, new_total, old_weighted * shrink[..., None] + added)
    final_top, final_total, final_weighted = running
    attended = (final_weighted / final_total[..., None]).astype(jnp.bfloat16)
    partial_value = jnp.einsum(
        "phqd,hde->pqe",
        attended,
        out_weight.reshape(local_heads, head_dim, model_width),
        preferred_element_type=jnp.float32,
    )
    reduced = lax.psum_scatter(
        partial_value.astype(jnp.bfloat16), "head", scatter_dimension=2, tiled=True
    ).astype(jnp.float32)
    gate_part = lax.dynamic_slice_in_dim(modulation[:, 2], head_seat * width_part, width_part, 1)
    result = (
        image_hidden.astype(jnp.float32)
        + gate_part[:, None, :] * reduced
        + cached_residual.astype(jnp.float32)
    )
    return result.astype(jnp.bfloat16)


def solution(mesh):
    in_specs = (
        P("batch", "seq", "head"),
        P("batch", None, None),
        P(None, None, "head"),
        P("head", None),
        P(),
        P(),
        P("batch", "seq", "head"),
        P("batch", "seq", "head"),
        P("batch", "seq", "head"),
        P("batch", "seq", "head"),
        P("batch", "seq", "head"),
        P("batch"),
        P("batch"),
        P("batch"),
    )
    out_specs = P("batch", "seq", "head")
    return jax.shard_map(
        per_device, mesh=mesh, in_specs=in_specs, out_specs=out_specs, check_vma=False
    )
```

profile of v0, /device:TPU:0, one launch (start us, length us, event | category | flops | bytes accessed | tf_op | source)
XLA Modules:
  0.0 229.3 jit_solution(13103266877624958867)
XLA Ops:
  7.3 18.8 %copy.40 = bf16[3072,3,768]{0,2,1:T(8,128)(2,1)} copy(bf16[3072,3,768]{2,0,1:T(8,128)(2,1)} %param.16) | data formatting | bytes 28311552 | tf_op args[2]
  28.6 1.2 copy.52
  30.5 1.2 copy.51
  33.0 23.5 %all-gather.6.cloned.1.call-done = bf16[2,256,3072]{2,1,0:T(8,128)(2,1)} async-done(((bf16[2,256,1536]{2,1,0:T(8,128)(2,1)}), bf16[2,256,3072]{2,1,0:T(8,128)(2,1)}) %all-gather.6.cloned.1.call-update) | async-done | bytes 3145744 | tf_op jit(solution)/shard_map/all_gather | solution.py:70
  56.5 2.5 %convert_reduce_fusion = f32[2,256]{1,0:T(2,128)S(1)} fusion(bf16[2,256,3072]{2,1,0:T(8,128)(2,1)} %all-gather.6.cloned.1.call-done), kind=kLoop, calls=%fused_computation.5 | loop fusion | flops 3145216 | bytes 3147776 | tf_op jit(solution)/shard_map/reduce_sum | solution.py:73
  59.4 1.0 fusion.4
  60.3 10.8 %fusion.13 = f32[2,256,3,6,128]{1,4,3,2,0:T(8,128)S(1)} fusion(bf16[3,6,128,3072,1]{3,2,1,0,4:T(8,128)(2,1)} %bitcast.73, bf16[2,256,3072]{2,1,0:T(8,128)(2,1)S(1)} %copy-done.2, f32[2,3072]{1,0:T(2,128)S(1)} %get-tuple-element.18, f32[2,3072]{1,0:T(2,128)S(1)} %get-tuple-element.19, f32[2,256]{1,0:T(2,128)S(1)} %add_rsqrt_fusion.2, ...), kind=kOutput, calls=%fused_computation.17 | convolution fusion | flops 7257194496 | bytes 22073344 | tf_op jit(solution)/shard_map/dot_general | solution.py:80
  71.5 1.8 copy-done.1
  74.0 1.6 copy.53
  75.6 1.3 mul.206
  76.8 3.1 %copy.50 = f32[2,256,768]{2,1,0:T(8,128)} copy(f32[2,256,768]{1,2,0:T(8,128)} %bitcast.80) | data formatting | bytes 3145728 | tf_op jit(solution)/shard_map/mul | solution.py:37
  79.9 1.6 copy.49
  81.5 4.8 %broadcast_select_fusion.3 = (bf16[2,256,768]{2,1,0:T(8,128)(2,1)}, bf16[2,256,768]{2,1,0:T(8,128)(2,1)}) fusion(bf16[2,256,768]{2,1,0:T(8,128)(2,1)} %param.22, pred[]{:T(512)S(6)} %eq.22, f32[2,256,768]{2,1,0:T(8,128)} %copy.53, f32[256,768]{1,0:T(8,128)} %copy.52, f32[256,768]{1,0:T(8,128)} %copy.51, f32[768]{0:T(1024)S(1)} %broadcast_bitcast_fusion, ...), kind=kLoop, calls=%fused_computation.54 | loop fusion | flops 2752512 | bytes 8653825 | tf_op jit(solution)/shard_map/jit(_where)/select_n | solution.py:120
  86.4 1.5 slice.60
  88.2 2.1 broadcast_select_fusion.2
  90.5 6.7 %all_gather.16 = bf16[2,128,768]{2,0,1:T(2,128)(2,1)} all-gather(bf16[2,32,768]{2,0,1:T(2,128)(2,1)S(1)} %copy.41), channel_id=1, replica_groups=mesh['batch'=4,'seq'=4,'head'=2] {'seq'}, dimensions={1}, use_global_device_ids=true | all-gather | bytes 491520 | tf_op jit(solution)/shard_map/all_gather | solution.py:98
  97.2 1.3 copy.42
  98.5 1.0 copy.45
  99.6 9.8 %all_gather.17 = bf16[2,128,768]{2,0,1:T(2,128)(2,1)} all-gather(bf16[2,32,768]{2,0,1:T(2,128)(2,1)S(1)} %copy.45), channel_id=1, replica_groups=mesh['batch'=4,'seq'=4,'head'=2] {'seq'}, dimensions={1}, use_global_device_ids=true | all-gather | bytes 491520 | tf_op jit(solution)/shard_map/all_gather | solution.py:99
  109.3 1.3 copy.46
  111.3 1.2 copy.54
  114.6 1.6 fusion.38
  116.9 3.2 %copy.55 = bf16[8,256,768]{1,2,0:T(8,128)(2,1)S(1)} copy(bf16[8,256,768]{2,1,0:T(8,128)(2,1)} %all-gather.8.cloned.1.call-done) | data formatting | bytes 6291456 | tf_op jit(solution)/shard_map/all_gather | solution.py:122
  120.0 26.9 %all-gather.10.cloned.1.call-done = bf16[8,256,768]{2,1,0:T(8,128)(2,1)} async-done(((bf16[2,256,768]{2,1,0:T(8,128)(2,1)}), bf16[8,256,768]{2,1,0:T(8,128)(2,1)}) %all-gather.10.cloned.1.call-update) | async-done | bytes 3145744 | tf_op jit(solution)/shard_map/all_gather | solution.py:123
  147.0 4.7 %copy.59 = bf16[8,256,768]{1,2,0:T(8,128)(2,1)} copy(bf16[8,256,768]{2,1,0:T(8,128)(2,1)} %all-gather.10.cloned.1.call-done) | data formatting | bytes 6291456 | tf_op jit(solution)/shard_map/all_gather | solution.py:123
  151.6 4.6 %broadcast_select_fusion.1 = (bf16[4,2,256,768]{2,3,1,0:T(8,128)(2,1)S(1)}, bf16[4,2,256,768]{2,3,1,0:T(8,128)(2,1)}) fusion(bf16[4,2,256,768]{2,3,1,0:T(8,128)(2,1)S(1)} %bitcast.75, pred[4]{0:T(512)(128)(4,1)S(1)} %copy-done.17, bf16[2,256,768]{1,2,0:T(8,128)(2,1)} %copy.54, bf16[4,2,256,768]{2,3,1,0:T(8,128)(2,1)} %bitcast.76, ...), kind=kLoop, calls=%fused_computation.27 | loop fusion | flops 3145728 | bytes 14155780 | tf_op jit(solution)/shard_map/jit(_where)/select_n | solution.py:126
  156.3 3.0 %multiply_reduce_fusion = (f32[2,6,256]{2,1,0:T(8,128)S(1)}, f32[2,6,256,4,256]{2,4,3,1,0:T(8,128)S(1)}) fusion(bf16[4,2,256,6,128]{2,4,3,1,0:T(8,128)(2,1)S(1)} %bitcast.74, bf16[2,256,6,128]{1,3,2,0:T(8,128)(2,1)} %copy-done.3), kind=kOutput, calls=%fused_computation.1 | convolution fusion | flops 811594752 | bytes 16527360 | tf_op jit(solution)/shard_map/pqhd,npkhd->phqnk/dot_general | solution.py:132
  159.3 2.1 fusion
  161.5 3.1 %copy-done = f32[2,6,256,4,256]{2,4,3,1,0:T(8,128)} copy-done((f32[2,6,256,4,256]{2,4,3,1,0:T(8,128)}, f32[2,6,256,4,256]{2,4,3,1,0:T(8,128)S(1)}, u32[]{:S(2)}) %copy-start) | copy-done | bytes 12582936
  164.6 11.3 %bitcast_convert_fusion = bf16[2,256,3072]{2,1,0:T(8,128)(2,1)} fusion(bf16[6,128,3072,1]{2,1,0,3:T(8,128)(2,1)} %bitcast.86, f32[2,6,256,128]{3,2,1,0:T(8,128)} %fusion.38, bf16[4,2,256,6,128]{2,4,3,1,0:T(8,128)(2,1)S(1)} %bitcast.83, f32[2,6,256,4,256]{2,4,3,1,0:T(8,128)} %copy-done, f32[2,6,256]{2,1,0:T(8,128)S(1)} %max.14, ...), kind=kOutput, calls=%fused_computation.13 | convolution fusion | flops 3233808384 | bytes 25202688 | tf_op jit(solution)/shard_map/phqd,hde->pqe/dot_general | solution.py:148
  176.0 43.5 %reduce-scatter.2.cloned.1.call-done = bf16[2,256,1536]{2,1,0:T(8,128)(2,1)} async-done(((bf16[2,256,3072]{2,1,0:T(8,128)(2,1)}), bf16[2,256,1536]{2,1,0:T(8,128)(2,1)}) %reduce-scatter.2.cloned.1.call-update) | async-done | bytes 1572880 | tf_op jit(solution)/shard_map/reduce_scatter | solution.py:154
  219.6 3.2 %add_convert_fusion = bf16[2,256,1536]{2,1,0:T(8,128)(2,1)} fusion(bf16[2,256,1536]{2,1,0:T(8,128)(2,1)S(1)} %copy-done.8, bf16[2,256,1536]{2,1,0:T(8,128)(2,1)} %reduce-scatter.2.cloned.1.call-done, bf16[2,256,1536]{2,1,0:T(8,128)(2,1)S(1)} %copy-done.5, f32[2,1536]{1,0:T(2,128)S(1)} %dynamic-slice_bitcast_fusion), kind=kLoop, calls=%fused_computation.21 | loop fusion | flops 5505024 | bytes 6303744 | tf_op jit(solution)/shard_map/convert_element_type | solution.py:163
  (83 shorter events, 9.1 us)
Async XLA Ops:
  6.5 50.0 %all-gather.6.cloned.1.call-start = ((), (), s32[]{:S(2)}) async-start(), calls=%async_computation.1 | async-start | bytes 4718592 | tf_op jit(solution)/shard_map/all_gather | solution.py:70
  7.3 109.6 %all-gather.8.cloned.1.call-start = ((), (), s32[]{:S(2)}) async-start(), calls=%async_computation.3 | async-start | bytes 3932160 | tf_op jit(solution)/shard_map/all_gather | solution.py:122
  7.3 18.8 %copy-start.18 = (s32[4]{0:T(128)S(1)}, s32[4]{0:T(128)}, u32[]{:S(2)}) copy-start(s32[4]{0:T(128)} %param.26) | copy-start | bytes 52
  7.3 18.8 %copy-start.19 = (s32[4]{0:T(128)S(1)}, s32[4]{0:T(128)}, u32[]{:S(2)}) copy-start(s32[4]{0:T(128)} %param.25) | copy-start | bytes 52
  26.1 6.2 %copy-start.16 = (f32[128]{0:T(128)S(1)}, f32[128]{0:T(128)}, u32[]{:S(2)}) copy-start(f32[128]{0:T(128)} %param.19) | copy-start | bytes 1540
  26.1 6.2 %copy-start.14 = (f32[2,3,3072]{2,0,1:T(2,128)S(1)}, f32[2,3,3072]{2,0,1:T(2,128)}, u32[]{:S(2)}) copy-start(f32[2,3,3072]{2,0,1:T(2,128)} %param.15) | copy-start | bytes 221188
  27.9 0.7 copy-start.9
  29.8 0.7 copy-start.11
  56.5 2.8 %copy-start.2 = (bf16[2,256,3072]{2,1,0:T(8,128)(2,1)S(1)}, bf16[2,256,3072]{2,1,0:T(8,128)(2,1)}, u32[]{:S(2)}) copy-start(bf16[2,256,3072]{2,1,0:T(8,128)(2,1)} %all-gather.6.cloned.1.call-done) | copy-start | bytes 9437188
  71.2 2.1 copy-start.1
  71.2 2.1 copy-start.20
  75.6 4.3 %slice-start = ((f32[2,256,3,6,128]{1,4,3,2,0:T(8,128)}), f32[2,256,1,6,128]{1,4,3,2,0:T(8,128)S(1)}, s32[]{:S(2)}) async-start(f32[2,256,3,6,128]{1,4,3,2,0:T(8,128)} %copy-done.1), calls=%async_computation.5 | async-start | bytes 3145728 | tf_op jit(solution)/shard_map/slice | solution.py:92
  86.3 4.1 %copy-start.13 = (bf16[2,32,768]{2,1,0:T(8,128)(2,1)S(1)}, bf16[2,32,768]{2,1,0:T(8,128)(2,1)}, u32[]{:S(2)}) copy-start(bf16[2,32,768]{2,1,0:T(8,128)(2,1)} %param.20) | copy-start | bytes 294916
  86.3 60.6 %all-gather.10.cloned.1.call-start = ((), (), s32[]{:S(2)}) async-start(), calls=%async_computation.4 | async-start | bytes 3932160 | tf_op jit(solution)/shard_map/all_gather | solution.py:123
  87.9 11.7 %copy-start.4 = (bf16[2,256,1,6,128]{1,4,3,2,0:T(8,128)(2,1)}, bf16[2,256,1,6,128]{1,4,3,2,0:T(8,128)(2,1)S(1)}, u32[]{:S(2)}) copy-start(bf16[2,256,1,6,128]{1,4,3,2,0:T(8,128)(2,1)S(1)} %slice.60) | copy-start | bytes 2359300
  88.2 23.1 %copy-start.21 = (s32[2]{0:T(128)S(1)}, s32[2]{0:T(128)}, u32[]{:S(2)}) copy-start(s32[2]{0:T(128)} %param.27) | copy-start | bytes 28
  90.3 21.0 %copy-start.7 = (bf16[2,256,768]{2,1,0:T(8,128)(2,1)S(1)}, bf16[2,256,768]{2,1,0:T(8,128)(2,1)}, u32[]{:S(2)}) copy-start(bf16[2,256,768]{2,1,0:T(8,128)(2,1)} %get-tuple-element.10) | copy-start | bytes 2359300
  90.3 129.2 %reduce-scatter.2.cloned.1.call-start = ((), (), s32[]{:S(2)}) async-start(), calls=%async_computation.2 | async-start | bytes 4718592 | tf_op jit(solution)/shard_map/reduce_scatter | solution.py:154
  109.3 3.3 %copy-start.10 = (f32[256,128]{0,1:T(8,128)S(1)}, f32[256,128]{0,1:T(8,128)}, u32[]{:S(2)}) copy-start(f32[256,128]{0,1:T(8,128)} %copy-done.9) | copy-start | bytes 393220
  109.3 3.4 %copy-start.12 = (f32[256,128]{0,1:T(8,128)S(1)}, f32[256,128]{0,1:T(8,128)}, u32[]{:S(2)}) copy-start(f32[256,128]{0,1:T(8,128)} %copy-done.11) | copy-start | bytes 393220
  113.1 0.9 copy-start.3
  120.0 31.6 %copy-start.17 = (pred[4]{0:T(512)(128)(4,1)S(1)}, pred[4]{0:T(512)(128)(4,1)}, u32[]{:S(2)}) copy-start(pred[4]{0:T(512)(128)(4,1)} %iota_compare_fusion.1) | copy-start | bytes 16
  159.3 5.3 %copy-start = (f32[2,6,256,4,256]{2,4,3,1,0:T(8,128)}, f32[2,6,256,4,256]{2,4,3,1,0:T(8,128)S(1)}, u32[]{:S(2)}) copy-start(f32[2,6,256,4,256]{2,4,3,1,0:T(8,128)S(1)} %get-tuple-element.28) | copy-start | bytes 37748740
  159.3 5.3 %copy-start.6 = (bf16[4,2,256,768]{2,3,1,0:T(8,128)(2,1)S(1)}, bf16[4,2,256,768]{2,3,1,0:T(8,128)(2,1)}, u32[]{:S(2)}) copy-start(bf16[4,2,256,768]{2,3,1,0:T(8,128)(2,1)} %get-tuple-element.24) | copy-start | bytes 9437188
  164.6 11.4 %copy-start.15 = (f32[2,1,3072]{2,0,1:T(2,128)S(1)}, f32[2,1,3072]{2,0,1:T(2,128)}, u32[]{:S(2)}) copy-start(f32[2,1,3072]{2,0,1:T(2,128)} %get-tuple-element.17) | copy-start | bytes 73732
  176.0 43.6 %copy-start.5 = (bf16[2,256,1536]{2,1,0:T(8,128)(2,1)S(1)}, bf16[2,256,1536]{2,1,0:T(8,128)(2,1)}, u32[]{:S(2)}) copy-start(bf16[2,256,1536]{2,1,0:T(8,128)(2,1)} %param.14) | copy-start | bytes 4718596
  176.0 43.6 %copy-start.8 = (bf16[2,256,1536]{2,1,0:T(8,128)(2,1)S(1)}, bf16[2,256,1536]{2,1,0:T(8,128)(2,1)}, u32[]{:S(2)}) copy-start(bf16[2,256,1536]{2,1,0:T(8,128)(2,1)} %param.24) | copy-start | bytes 4718596
Sparse Core Ops, SparseCore 0:
  8.9 47.6 all-gather.5
  86.4 30.3 all-gather.7
  118.4 28.4 all-gather.9
  176.1 43.3 reduce-scatter.1
where the time goes:
time: 230 us; the launch traced here: 229 us
  waiting for transfers between devices  95.4 us (41%)
  local copies, waits for them, and re-layouts  51.2 us (22%)
  matrix products  27.2 us (12%)
  other arithmetic  24.2 us (11%)
  blocking collectives  16.5 us (7%)
  between operations  14.8 us (6%)
    reduce_scatter x1, waiting for transfers between devices, per_device(): lax.psum_scatter(partial_value.astype(jnp.bfloat16), 'head', scatter_dime...  43.5 us
    unnamed x47, local copies, waits for them, and re-layouts  27.4 us
    all_gather x1, waiting for transfers between devices, per_device(): value_rows = lax.all_gather(chosen_v[None], 'seq', axis=0, tiled=True)  26.9 us
    all_gather x1, waiting for transfers between devices, per_device(): gathered = lax.all_gather(image_hidden, 'head', axis=2, tiled=True)  23.5 us
    dot_general x1, matrix products, per_device(): jnp.einsum('phqd,hde->pqe', attended, out_weight.reshape(local_heads, hea...  11.3 us
    dot_general x1, matrix products, per_device(): jnp.dot(modulated.reshape(prompts * tok_rows, model_width), qkv_weight.re...  10.8 us
    all_gather x1, blocking collectives, per_device(): lax.all_gather(text_values, 'seq', axis=1, tiled=True)  9.76 us
    all_gather x1, blocking collectives, per_device(): lax.all_gather(text_keys, 'seq', axis=1, tiled=True)  6.72 us
  transfers between devices with their start and end apart: 4, of which 4 were waited for; matrix products, arithmetic and copies ran while one was open for 17% of the time, Pallas kernels for 0%

commit v1 on v0

--- a/solution.py
+++ b/solution.py
@@ -1,3 +1,4 @@
+import functools
 import jax
 import jax.numpy as jnp
 from jax import lax
@@ -5,6 +6,34 @@
 
 GRID_W = 64
 epsilon = 1e-06
+
+
+def cubes_produce(my_data, ndim_at):
+    latest = jax.lax.axis_size("seq")
+    local_now = jax.lax.axis_index("seq")
+    passed, outcome_arr, vec_out = (latest, local_now, my_data.shape[ndim_at])
+    sides = []
+    for tick, dev in enumerate(my_data.shape):
+        sides.append(dev * passed if tick == ndim_at else dev)
+    current_value = lax.dynamic_update_slice_in_dim(
+        jnp.zeros(sides, my_data.dtype), my_data, outcome_arr * vec_out, axis=ndim_at
+    )
+    j0 = 1
+    while j0 < passed:
+        panels = []
+        tick = 0
+        while tick < passed:
+            panels.append((tick, (tick + 1) % passed))
+            tick += 1
+        my_data = jax.lax.ppermute(my_data, axis_name="seq", perm=panels)
+        current_value = lax.dynamic_update_slice_in_dim(
+            current_value, my_data, (outcome_arr - j0) % passed * vec_out, axis=ndim_at
+        )
+        j0 += 1
+    return current_value
+
+
+edge_bind = functools.partial(cubes_produce, ndim_at=1)
 
 
 def rotary_tables(raster, head_dim, grid_width):
@@ -94,10 +123,7 @@
     fresh_k_flat = fresh_k.reshape(prompts, tok_rows, channels)
     fresh_v_flat = fresh_v.reshape(prompts, tok_rows, channels)
     score_scale = head_dim ** (-0.5)
-    text_k, text_v = (
-        lax.all_gather(text_keys, "seq", axis=1, tiled=True),
-        lax.all_gather(text_values, "seq", axis=1, tiled=True),
-    )
+    text_k, text_v = (lax.all_gather(text_keys, "seq", axis=1, tiled=True), edge_bind(text_values))
     total_text = text_k.shape[1]
     text_key_rows = text_k.reshape(prompts, total_text, local_heads, head_dim)
     text_value_rows = text_v.reshape(prompts, total_text, local_heads, head_dim)

time: 230 us -> 246 us (1.070)
  local copies, waits for them, and re-layouts: 51.2 us -> 77.8 us
  waiting for transfers between devices: 95.4 us -> 78 us
  blocking collectives: 16.5 us -> 19.2 us
    all_gather x1, waiting for transfers between devices: 26.9 us -> 0.01 us  [per_device(): value_rows = lax.all_gather(chosen_v[None], 'seq', axis=0, tiled=True)]
    dynamic_update_slice x0 -> x4, local copies, waits for them, and re-layouts: none -> 24 us  [the longest x3 18.8 us: cubes_produce(): lax.dynamic_update_slice_in_dim(current_value, my_data, (outcome_arr - j0...]
    all_gather x1, blocking collectives: 6.72 us -> 19.2 us  [per_device(): lax.all_gather(text_keys, 'seq', axis=1, tiled=True)]
    ppermute x0 -> x3, waiting for transfers between devices: none -> 10.5 us  [cubes_produce(): my_data = jax.lax.ppermute(my_data, axis_name='seq', perm=panels)]
    all_gather x1 -> x0, blocking collectives: 9.76 us -> none  [per_device(): lax.all_gather(text_values, 'seq', axis=1, tiled=True)]
    dot_general x1, matrix products: 1.59 us -> 6.27 us  [per_device(): jnp.einsum('phqnk,npkhd->phqd', weights.astype(jnp.bfloat16), value_rows,...]
    dot_general x1, matrix products: 11.3 us -> 7.14 us  [per_device(): jnp.einsum('phqd,hde->pqe', attended, out_weight.reshape(local_heads, hea...]
    unnamed x47 -> x55, local copies, waits for them, and re-layouts: 27.4 us -> 28.9 us
  transfers between devices with their start and end apart: 4 -> 7, of which waited for: 4 -> 3; matrix products, arithmetic and copies ran while one was open for 17% -> 26% of each run, Pallas kernels for 0% -> 0%
where the time goes in v1:
time: 246 us; the launch traced here: 244 us
  waiting for transfers between devices  78 us (32%)
  local copies, waits for them, and re-layouts  77.8 us (32%)
  matrix products  27.7 us (11%)
  other arithmetic  25.1 us (10%)
  blocking collectives  19.2 us (8%)
  between operations  15 us (6%)
    reduce_scatter x1, waiting for transfers between devices, per_device(): lax.psum_scatter(partial_value.astype(jnp.bfloat16), 'head', scatter_dime...  43.2 us
    unnamed x55, local copies, waits for them, and re-layouts  28.9 us
    all_gather x1, waiting for transfers between devices, per_device(): gathered = lax.all_gather(image_hidden, 'head', axis=2, tiled=True)  23.6 us
    all_gather x1, blocking collectives, per_device(): lax.all_gather(text_keys, 'seq', axis=1, tiled=True)  19.2 us
    dynamic_update_slice x3, local copies, waits for them, and re-layouts, cubes_produce(): lax.dynamic_update_slice_in_dim(current_value, my_data, (outcome_arr - j0...  18.8 us
    dot_general x1, matrix products, per_device(): jnp.dot(modulated.reshape(prompts * tok_rows, model_width), qkv_weight.re...  10.8 us
    ppermute x3, waiting for transfers between devices, cubes_produce(): my_data = jax.lax.ppermute(my_data, axis_name='seq', perm=panels)  10.5 us
    dot_general x1, matrix products, per_device(): jnp.einsum('phqd,hde->pqe', attended, out_weight.reshape(local_heads, hea...  7.14 us
  transfers between devices with their start and end apart: 7, of which 3 were waited for; matrix products, arithmetic and copies ran while one was open for 26% of the time, Pallas kernels for 0%

profile of v1, /device:TPU:0, one launch (start us, length us, event | category | flops | bytes accessed | tf_op | source)
XLA Modules:
  0.0 244.3 jit_solution(16612939220886836626)
XLA Ops:
  7.3 18.8 %copy.41 = bf16[3072,3,768]{0,2,1:T(8,128)(2,1)} copy(bf16[3072,3,768]{2,0,1:T(8,128)(2,1)} %param.16) | data formatting | bytes 28311552 | tf_op args[2]
  33.0 23.6 %all-gather.6.cloned.1.call-done = bf16[2,256,3072]{2,1,0:T(8,128)(2,1)} async-done(((bf16[2,256,1536]{2,1,0:T(8,128)(2,1)}), bf16[2,256,3072]{2,1,0:T(8,128)(2,1)}) %all-gather.6.cloned.1.call-update) | async-done | bytes 3145744 | tf_op jit(solution)/shard_map/all_gather | solution.py:99
  56.5 2.5 %convert_reduce_fusion = f32[2,256]{1,0:T(2,128)S(1)} fusion(bf16[2,256,3072]{2,1,0:T(8,128)(2,1)} %all-gather.6.cloned.1.call-done), kind=kLoop, calls=%fused_computation.5 | loop fusion | flops 3145216 | bytes 3147776 | tf_op jit(solution)/shard_map/reduce_sum | solution.py:102
  60.3 10.8 %fusion.13 = f32[2,256,3,6,128]{1,4,3,2,0:T(8,128)S(1)} fusion(bf16[3,6,128,3072,1]{3,2,1,0,4:T(8,128)(2,1)} %bitcast.73, bf16[2,256,3072]{2,1,0:T(8,128)(2,1)S(1)} %copy-done.2, f32[2,3072]{1,0:T(2,128)S(1)} %get-tuple-element.18, f32[2,3072]{1,0:T(2,128)S(1)} %get-tuple-element.19, f32[2,256]{1,0:T(2,128)S(1)} %add_rsqrt_fusion.2, ...), kind=kOutput, calls=%fused_computation.17 | convolution fusion | flops 7257194496 | bytes 22073344 | tf_op jit(solution)/shard_map/dot_general | solution.py:109
  71.5 1.8 copy-done.1
  74.0 1.6 copy.54
  75.6 1.3 mul.222
  76.8 3.1 %copy.51 = f32[2,256,768]{2,1,0:T(8,128)} copy(f32[2,256,768]{1,2,0:T(8,128)} %bitcast.81) | data formatting | bytes 3145728 | tf_op jit(solution)/shard_map/mul | solution.py:66
  79.9 1.6 copy.50
  81.5 4.8 %broadcast_select_fusion.3 = (bf16[2,256,768]{2,1,0:T(8,128)(2,1)}, bf16[2,256,768]{2,1,0:T(8,128)(2,1)}) fusion(bf16[2,256,768]{2,1,0:T(8,128)(2,1)} %param.22, pred[]{:T(512)S(6)} %eq.26, f32[2,256,768]{2,1,0:T(8,128)} %copy.54, f32[256,768]{1,0:T(8,128)} %copy.53, f32[256,768]{1,0:T(8,128)} %copy.52, f32[768]{0:T(1024)S(1)} %broadcast_bitcast_fusion, ...), kind=kLoop, calls=%fused_computation.53 | loop fusion | flops 2752512 | bytes 8653825 | tf_op jit(solution)/shard_map/jit(_where)/select_n | solution.py:146
  86.4 1.5 slice.60
  88.2 2.1 broadcast_select_fusion.2
  90.4 1.2 copy.46
  93.3 10.5 %collective-permute-done = bf16[2,32,768]{1,2,0:T(8,128)(2,1)} collective-permute-done((bf16[2,32,768]{1,2,0:T(8,128)(2,1)S(1)}, bf16[2,32,768]{1,2,0:T(8,128)(2,1)}, u32[]{:S(2)}, u32[]{:S(2)}) %collective-permute-start) | collective-permute-done | bytes 98336 | tf_op jit(solution)/shard_map/ppermute | solution.py:28
  103.7 19.2 %all_gather.13 = bf16[2,128,768]{2,0,1:T(2,128)(2,1)} all-gather(bf16[2,32,768]{2,0,1:T(2,128)(2,1)S(1)} %copy.42), channel_id=1, replica_groups=mesh['batch'=4,'seq'=4,'head'=2] {'seq'}, dimensions={1}, use_global_device_ids=true | all-gather | bytes 491520 | tf_op jit(solution)/shard_map/all_gather | solution.py:126
  122.9 1.3 copy.43
  124.3 5.2 %dynamic_update_slice.12 = bf16[2,128,768]{1,2,0:T(8,128)(2,1)S(1)} dynamic-update-slice(bf16[2,128,768]{1,2,0:T(8,128)(2,1)S(1)} %broadcast_in_dim.109, bf16[2,32,768]{1,2,0:T(8,128)(2,1)} %copy-done.10, s32[]{:T(128)} %constant.84.clone.1, s32[]{:T(128)S(6)} %select_n.107, s32[]{:T(128)} %constant.84.clone.1) | dynamic-update-slice | bytes 196612 | tf_op jit(solution)/shard_map/dynamic_update_slice | solution.py:18
  129.6 1.4 collective-permute-start.2
  131.6 6.2 %dynamic_update_slice.13 = bf16[2,128,768]{1,2,0:T(8,128)(2,1)S(1)} dynamic-update-slice(bf16[2,128,768]{1,2,0:T(8,128)(2,1)S(1)} %dynamic_update_slice.12, bf16[2,32,768]{1,2,0:T(8,128)(2,1)} %collective-permute-done, s32[]{:T(128)} %constant.84.clone.1, s32[]{:T(128)S(6)} %select_n.109, s32[]{:T(128)} %constant.84.clone.1) | dynamic-update-slice | bytes 196612 | tf_op jit(solution)/shard_map/dynamic_update_slice | solution.py:29
  137.8 6.3 %dynamic_update_slice.14 = bf16[2,128,768]{1,2,0:T(8,128)(2,1)S(1)} dynamic-update-slice(bf16[2,128,768]{1,2,0:T(8,128)(2,1)S(1)} %dynamic_update_slice.13, bf16[2,32,768]{1,2,0:T(8,128)(2,1)} %collective-permute-done.1, s32[]{:T(128)} %constant.84.clone.1, s32[]{:T(128)S(6)} %select_n.111, s32[]{:T(128)} %constant.84.clone.1) | dynamic-update-slice | bytes 196612 | tf_op jit(solution)/shard_map/dynamic_update_slice | solution.py:29
  144.2 6.3 %dynamic_update_slice.15 = bf16[2,128,768]{1,2,0:T(8,128)(2,1)S(1)} dynamic-update-slice(bf16[2,128,768]{1,2,0:T(8,128)(2,1)S(1)} %dynamic_update_slice.14, bf16[2,32,768]{1,2,0:T(8,128)(2,1)} %collective-permute-done.2, s32[]{:T(128)} %constant.84.clone.1, s32[]{:T(128)S(6)} %select_n.113, s32[]{:T(128)} %constant.84.clone.1) | dynamic-update-slice | bytes 196612 | tf_op jit(solution)/shard_map/dynamic_update_slice | solution.py:29
  150.5 1.2 copy.55
  155.6 4.7 %copy.56 = bf16[8,256,768]{1,2,0:T(8,128)(2,1)} copy(bf16[8,256,768]{2,1,0:T(8,128)(2,1)} %all-gather.8.cloned.1.call-done) | data formatting | bytes 6291456 | tf_op jit(solution)/shard_map/all_gather | solution.py:148
  160.3 4.7 %copy.60 = bf16[8,256,768]{1,2,0:T(8,128)(2,1)} copy(bf16[8,256,768]{2,1,0:T(8,128)(2,1)} %all-gather.10.cloned.1.call-done) | data formatting | bytes 6291456 | tf_op jit(solution)/shard_map/all_gather | solution.py:149
  164.9 3.9 %broadcast_select_fusion = (bf16[4,2,256,768]{2,3,1,0:T(8,128)(2,1)S(1)}, bf16[4,2,256,768]{2,3,1,0:T(8,128)(2,1)S(1)}) fusion(bf16[4,2,256,768]{2,3,1,0:T(8,128)(2,1)} %bitcast.77, pred[4]{0:T(512)(128)(4,1)S(1)} %copy-done.21, bf16[2,256,768]{1,2,0:T(8,128)(2,1)} %bitcast.79, bf16[4,2,256,768]{2,3,1,0:T(8,128)(2,1)} %bitcast.76, bf16[2,256,768]{1,2,0:T(8,128)(2,1)} %copy.55), kind=kLoop, calls=%fused_computation.26 | loop fusion | flops 3145728 | bytes 14155780 | tf_op jit(solution)/shard_map/jit(_where)/select_n | solution.py:153
  168.9 3.0 %multiply_reduce_fusion = (f32[2,6,256]{2,1,0:T(8,128)S(1)}, f32[2,6,256,4,256]{2,4,3,1,0:T(8,128)S(1)}) fusion(bf16[4,2,256,6,128]{2,4,3,1,0:T(8,128)(2,1)S(1)} %bitcast.75, bf16[2,256,6,128]{1,3,2,0:T(8,128)(2,1)} %copy-done.3), kind=kOutput, calls=%fused_computation.1 | convolution fusion | flops 811594752 | bytes 16527360 | tf_op jit(solution)/shard_map/pqhd,npkhd->phqnk/dot_general | solution.py:158
  171.9 2.1 fusion
  173.9 2.4 copy-done
  176.4 6.3 %fusion.8 = f32[2,6,256,128,1]{3,2,4,1,0:T(8,128)S(1)} fusion(f32[2,6,256,4,256]{2,4,3,1,0:T(8,128)} %copy-done, f32[2,6,256]{2,1,0:T(8,128)S(1)} %max.14, bf16[4,2,256,6,128]{2,4,3,1,0:T(8,128)(2,1)S(1)} %bitcast.74), kind=kOutput, calls=%fused_computation.12 | convolution fusion | flops 814743552 | bytes 17313792 | tf_op jit(solution)/shard_map/phqnk,npkhd->phqd/dot_general | solution.py:165
  183.3 7.1 %bitcast_convert_fusion = bf16[2,256,3072]{2,1,0:T(8,128)(2,1)} fusion(bf16[6,128,3072,1]{2,1,0,3:T(8,128)(2,1)} %bitcast.86, f32[2,6,256,128,1]{3,2,4,1,0:T(8,128)S(1)} %fusion.8, bf16[2,128,6,128]{1,3,2,0:T(8,128)(2,1)S(1)} %bitcast.85, f32[2,6,256,128]{2,3,1,0:T(8,128)S(1)} %copy-done.6, f32[2,6,256]{2,1,0:T(8,128)} %get-tuple-element.7, ...), kind=kOutput, calls=%fused_computation.13 | convolution fusion | flops 2520514560 | bytes 11440128 | tf_op jit(solution)/shard_map/phqd,hde->pqe/dot_general | solution.py:174
  191.3 43.2 %reduce-scatter.2.cloned.1.call-done = bf16[2,256,1536]{2,1,0:T(8,128)(2,1)} async-done(((bf16[2,256,3072]{2,1,0:T(8,128)(2,1)}), bf16[2,256,1536]{2,1,0:T(8,128)(2,1)}) %reduce-scatter.2.cloned.1.call-update) | async-done | bytes 1572880 | tf_op jit(solution)/shard_map/reduce_scatter | solution.py:180
  234.6 3.2 %add_convert_fusion = bf16[2,256,1536]{2,1,0:T(8,128)(2,1)} fusion(bf16[2,256,1536]{2,1,0:T(8,128)(2,1)S(1)} %copy-done.9, bf16[2,256,1536]{2,1,0:T(8,128)(2,1)} %reduce-scatter.2.cloned.1.call-done, bf16[2,256,1536]{2,1,0:T(8,128)(2,1)S(1)} %copy-done.7, f32[2,1536]{1,0:T(2,128)S(1)} %dynamic-slice_bitcast_fusion), kind=kLoop, calls=%fused_computation.21 | loop fusion | flops 5505024 | bytes 6303744 | tf_op jit(solution)/shard_map/convert_element_type | solution.py:189
  (100 shorter events, 16.6 us)
Async XLA Ops:
  6.5 50.0 %all-gather.6.cloned.1.call-start = ((), (), s32[]{:S(2)}) async-start(), calls=%async_computation.1 | async-start | bytes 4718592 | tf_op jit(solution)/shard_map/all_gather | solution.py:99
  7.3 148.3 %all-gather.8.cloned.1.call-start = ((), (), s32[]{:S(2)}) async-start(), calls=%async_computation.3 | async-start | bytes 3932160 | tf_op jit(solution)/shard_map/all_gather | solution.py:148
  7.3 18.8 %copy-start.22 = (s32[4]{0:T(128)S(1)}, s32[4]{0:T(128)}, u32[]{:S(2)}) copy-start(s32[4]{0:T(128)} %param.26) | copy-start | bytes 52
  7.3 18.8 %copy-start.23 = (s32[4]{0:T(128)S(1)}, s32[4]{0:T(128)}, u32[]{:S(2)}) copy-start(s32[4]{0:T(128)} %param.25) | copy-start | bytes 52
  26.1 6.2 %copy-start.19 = (f32[128]{0:T(128)S(1)}, f32[128]{0:T(128)}, u32[]{:S(2)}) copy-start(f32[128]{0:T(128)} %param.19) | copy-start | bytes 1540
  26.1 6.2 %copy-start.17 = (f32[2,3,3072]{2,0,1:T(2,128)S(1)}, f32[2,3,3072]{2,0,1:T(2,128)}, u32[]{:S(2)}) copy-start(f32[2,3,3072]{2,0,1:T(2,128)} %param.15) | copy-start | bytes 221188
  56.5 2.8 %copy-start.2 = (bf16[2,256,3072]{2,1,0:T(8,128)(2,1)S(1)}, bf16[2,256,3072]{2,1,0:T(8,128)(2,1)}, u32[]{:S(2)}) copy-start(bf16[2,256,3072]{2,1,0:T(8,128)(2,1)} %all-gather.6.cloned.1.call-done) | copy-start | bytes 9437188
  71.2 2.1 copy-start.1
  71.2 2.1 copy-start.24
  75.6 4.3 %slice-start = ((f32[2,256,3,6,128]{1,4,3,2,0:T(8,128)}), f32[2,256,1,6,128]{1,4,3,2,0:T(8,128)S(1)}, s32[]{:S(2)}) async-start(f32[2,256,3,6,128]{1,4,3,2,0:T(8,128)} %copy-done.1), calls=%async_computation.5 | async-start | bytes 3145728 | tf_op jit(solution)/shard_map/slice | solution.py:121
  86.3 5.3 %copy-start.25 = (s32[2]{0:T(128)S(1)}, s32[2]{0:T(128)}, u32[]{:S(2)}) copy-start(s32[2]{0:T(128)} %param.27) | copy-start | bytes 28
  86.3 74.0 %all-gather.10.cloned.1.call-start = ((), (), s32[]{:S(2)}) async-start(), calls=%async_computation.4 | async-start | bytes 3932160 | tf_op jit(solution)/shard_map/all_gather | solution.py:149
  87.9 36.4 %copy-start.4 = (bf16[2,256,1,6,128]{1,4,3,2,0:T(8,128)(2,1)}, bf16[2,256,1,6,128]{1,4,3,2,0:T(8,128)(2,1)S(1)}, u32[]{:S(2)}) copy-start(bf16[2,256,1,6,128]{1,4,3,2,0:T(8,128)(2,1)S(1)} %slice.60) | copy-start | bytes 2359300
  90.3 60.2 %copy-start.8 = (bf16[2,256,768]{2,1,0:T(8,128)(2,1)S(1)}, bf16[2,256,768]{2,1,0:T(8,128)(2,1)}, u32[]{:S(2)}) copy-start(bf16[2,256,768]{2,1,0:T(8,128)(2,1)} %get-tuple-element.10) | copy-start | bytes 2359300
  90.3 144.3 %reduce-scatter.2.cloned.1.call-start = ((), (), s32[]{:S(2)}) async-start(), calls=%async_computation.2 | async-start | bytes 4718592 | tf_op jit(solution)/shard_map/reduce_scatter | solution.py:180
  91.5 12.2 %copy-start.10 = (bf16[2,32,768]{1,2,0:T(8,128)(2,1)}, bf16[2,32,768]{1,2,0:T(8,128)(2,1)S(1)}, u32[]{:S(2)}) copy-start(bf16[2,32,768]{1,2,0:T(8,128)(2,1)S(1)} %copy.46) | copy-start | bytes 294916
  91.5 12.2 %collective-permute-start = (bf16[2,32,768]{1,2,0:T(8,128)(2,1)S(1)}, bf16[2,32,768]{1,2,0:T(8,128)(2,1)}, u32[]{:S(2)}, u32[]{:S(2)}) collective-permute-start(bf16[2,32,768]{1,2,0:T(8,128)(2,1)S(1)} %copy.46), channel_id=1, source_target_pairs={{0,2},{2,4},{4,6},{6,0},{1,3},{3,5},{5,7},{7,1},{8,10},{10,12},{12... | collective-permute-start | bytes 294920 | tf_op jit(solution)/shard_map/ppermute | solution.py:28
  103.7 25.8 %collective-permute-start.1 = (bf16[2,32,768]{1,2,0:T(8,128)(2,1)}, bf16[2,32,768]{1,2,0:T(8,128)(2,1)}, u32[]{:S(2)}, u32[]{:S(2)}) collective-permute-start(bf16[2,32,768]{1,2,0:T(8,128)(2,1)} %collective-permute-done), channel_id=1, source_target_pairs={{0,2},{2,4},{4,6},{6,0},{1,3},{3,5},{5,7},{7,1},{8,10},{10,12},{12... | collective-permute-start | bytes 294920 | tf_op jit(solution)/shard_map/ppermute | solution.py:28
  129.6 14.6 %collective-permute-start.2 = (bf16[2,32,768]{1,2,0:T(8,128)(2,1)}, bf16[2,32,768]{1,2,0:T(8,128)(2,1)}, u32[]{:S(2)}, u32[]{:S(2)}) collective-permute-start(bf16[2,32,768]{1,2,0:T(8,128)(2,1)} %collective-permute-done.1), channel_id=1, source_target_pairs={{0,2},{2,4},{4,6},{6,0},{1,3},{3,5},{5,7},{7,1},{8,10},{10,12},{12... | collective-permute-start | bytes 294920 | tf_op jit(solution)/shard_map/ppermute | solution.py:28
  137.8 14.0 %copy-start.12 = (f32[256,128]{0,1:T(8,128)S(1)}, f32[256,128]{0,1:T(8,128)}, u32[]{:S(2)}) copy-start(f32[256,128]{0,1:T(8,128)} %copy-done.11) | copy-start | bytes 393220
  137.8 14.0 %copy-start.14 = (f32[256,128]{0,1:T(8,128)S(1)}, f32[256,128]{0,1:T(8,128)}, u32[]{:S(2)}) copy-start(f32[256,128]{0,1:T(8,128)} %copy-done.13) | copy-start | bytes 393220
  150.4 1.8 copy-start.15
  151.6 1.5 copy-start.20
  152.2 0.9 copy-start.3
  153.6 1.1 copy-start.5
  160.3 4.7 %copy-start.21 = (pred[4]{0:T(512)(128)(4,1)S(1)}, pred[4]{0:T(512)(128)(4,1)}, u32[]{:S(2)}) copy-start(pred[4]{0:T(512)(128)(4,1)} %iota_compare_fusion.1) | copy-start | bytes 16
  171.9 4.5 %copy-start = (f32[2,6,256,4,256]{2,4,3,1,0:T(8,128)}, f32[2,6,256,4,256]{2,4,3,1,0:T(8,128)S(1)}, u32[]{:S(2)}) copy-start(f32[2,6,256,4,256]{2,4,3,1,0:T(8,128)S(1)} %get-tuple-element.28) | copy-start | bytes 37748740
  176.4 6.3 %copy-start.18 = (f32[2,6,256]{2,1,0:T(8,128)S(1)}, f32[2,6,256]{2,1,0:T(8,128)}, u32[]{:S(2)}) copy-start(f32[2,6,256]{2,1,0:T(8,128)} %fusion.28) | copy-start | bytes 36868
  176.4 6.9 %copy-start.6 = (f32[2,6,256,128]{2,3,1,0:T(8,128)S(1)}, f32[2,6,256,128]{2,3,1,0:T(8,128)}, u32[]{:S(2)}) copy-start(f32[2,6,256,128]{2,3,1,0:T(8,128)} %copy-done.5) | copy-start | bytes 4718596
  176.4 6.9 %copy-start.16 = (bf16[2,128,768]{1,2,0:T(8,128)(2,1)S(1)}, bf16[2,128,768]{1,2,0:T(8,128)(2,1)}, u32[]{:S(2)}) copy-start(bf16[2,128,768]{1,2,0:T(8,128)(2,1)} %copy-done.15) | copy-start | bytes 1179652
  190.4 44.1 %copy-start.7 = (bf16[2,256,1536]{2,1,0:T(8,128)(2,1)S(1)}, bf16[2,256,1536]{2,1,0:T(8,128)(2,1)}, u32[]{:S(2)}) copy-start(bf16[2,256,1536]{2,1,0:T(8,128)(2,1)} %param.14) | copy-start | bytes 4718596
  190.4 44.1 %copy-start.9 = (bf16[2,256,1536]{2,1,0:T(8,128)(2,1)S(1)}, bf16[2,256,1536]{2,1,0:T(8,128)(2,1)}, u32[]{:S(2)}) copy-start(bf16[2,256,1536]{2,1,0:T(8,128)(2,1)} %param.24) | copy-start | bytes 4718596
  (2 other events, 1.3 us)
Sparse Core Ops, SparseCore 0:
  8.9 47.6 all-gather.5
  86.4 36.1 all-gather.7
  124.2 31.3 all-gather.9
  190.6 43.9 reduce-scatter.1
